TPU v7x, 32 devices: a whole 2x2x4 slice. The times are simulated.
32 devices in a mesh: dp: 16 (over z, y, core), chan: 2 (over x).
Axes of the slice: x: 2, y: 2, z: 4, core: 2. Of those that a mesh axis runs over, the one named last changes fastest.
Arguments:
- inputs: bfloat16 [768, 196, 1024], P('dp', None, 'chan'), may hold values from -6 to 6
- norm_gain: float32 [1024], P('chan'), may hold values from 0.5 to 1.5
- norm_bias: float32 [1024], P('chan'), may hold values from -3 to 3
- w_first: bfloat16 [512, 196], replicated, may hold values from -0.4375 to 0.4375
- b_first: float32 [512], replicated, may hold values from -3 to 3
- w_second: bfloat16 [196, 512], replicated, may hold values from -0.25 to 0.25
- upstream: bfloat16 [768, 196, 1024], P('dp', None, 'chan'), may hold values from -6 to 6
Outputs:
- grad_input: bfloat16 [768, 196, 1024], P('dp', None, 'chan')
- grad_first: float32 [512, 196], P('dp')
- grad_second: float32 [196, 512], P(None, 'dp')
- grad_bias_first: float32 [512], P('dp')
- grad_gain: float32 [1024], P('chan')
- grad_shift: float32 [1024], P('chan')
All inputs are finite; a program needn't handle non-finite values.
Results may differ from a plain program's by a relative error of at most 0.0056.
Values sent between devices are 32-bit elements; how exact they have to be, the bound alone decides.
A program may use at most 192 MiB of HBM per device.

v0:
```python
import functools

import jax
import jax.numpy as jnp
from jax import lax
from jax.experimental import pallas as pl
from jax.experimental.pallas import tpu as pltpu
from jax.sharding import PartitionSpec as P

epsilon = 1e-06
T = 16
LANES = 256
MIB = 2**20


def column(lane, p, value, held):
    return jnp.where(lane == p, value, held)


def stats_kernel(x_ref, out_ref):
    i = pl.program_id(0)
    chans = x_ref.shape[2]
    images = x_ref.shape[1]
    lane = lax.broadcasted_iota(jnp.int32, (images, out_ref.shape[2]), 1)

    @pl.when(i == 0)
    def _():
        out_ref[...] = jnp.zeros_like(out_ref)

    means, squares = out_ref[0], out_ref[1]
    for j in range(T):
        x = x_ref[j].astype(jnp.float32)
        mean = jnp.sum(x, axis=-1, keepdims=True) * (1.0 / chans)
        d = x - mean
        square = jnp.sum(d * d, axis=-1, keepdims=True)
        means = column(lane, i * T + j, mean, means)
        squares = column(lane, i * T + j, square, squares)
    out_ref[0] = means
    out_ref[1] = squares


def main_kernel(
    patches,
    x_ref,
    up_ref,
    stat_ref,
    gain_ref,
    bias_ref,
    w1_ref,
    w1t_ref,
    w2t_ref,
    gm_ref,
    sums_ref,
    gf_ref,
    gs_ref,
    chan_ref,
    mixed,
    upper,
    gmix,
):
    g = pl.program_id(0)
    images, width = stat_ref.shape[1], stat_ref.shape[2]
    chans = x_ref.shape[2]
    hidden = w1_ref.shape[0]
    padded = w1_ref.shape[1]
    full, tail = patches // T, patches % T
    f32 = jnp.float32

    @pl.when(g == 0)
    def _():
        gf_ref[...] = jnp.zeros_like(gf_ref)
        gs_ref[...] = jnp.zeros_like(gs_ref)
        chan_ref[...] = jnp.zeros_like(chan_ref)

    gain = gain_ref[...]
    bias = bias_ref[...]

    def prepare(first, count, mean, inv):
        rows = []
        for j in range(count):
            x = x_ref[first + j].astype(f32)
            normed = (x - mean[:, j : j + 1]) * inv[:, j : j + 1]
            rows.append((normed * gain + bias).astype(jnp.bfloat16))
        return rows

    def rolled(i, which):
        return pltpu.roll(stat_ref[which], lax.rem(width - i * T, width), 1)

    def step(i, _):
        first = pl.multiple_of(i * T, T)
        rows = prepare(first, T, rolled(i, 0), rolled(i, 1))
        mixed[:, pl.ds(first, T), :] = jnp.swapaxes(jnp.stack(rows), 0, 1)
        upper[:, pl.ds(first, T), :] = jnp.swapaxes(up_ref[pl.ds(first, T)], 0, 1)
        return 0

    lax.fori_loop(0, full, step, 0)
    start = full * T
    one = jnp.ones((images, chans), jnp.bfloat16)
    zero = jnp.zeros((images, chans), jnp.bfloat16)
    rows = prepare(start, tail, stat_ref[0, :, start:], stat_ref[1, :, start:]) + [one] * 3
    rows = rows + [zero] * (padded - start - len(rows))
    mixed[:, start:padded, :] = jnp.swapaxes(jnp.stack(rows), 0, 1)
    ups = [up_ref[start + j] for j in range(tail)]
    ups = ups + [zero] * (padded - start - tail)
    upper[:, start:padded, :] = jnp.swapaxes(jnp.stack(ups), 0, 1)

    block = 256
    across = (((1,), (1,)), ((), ()))

    def image(b, _):
        mb = mixed[b]
        ub = upper[b]
        total = None
        for k in range(0, hidden, block):
            ks = slice(k, k + block)
            pre = jnp.dot(w1_ref[ks, :], mb, preferred_element_type=f32)
            cdf = 0.5 * (1.0 + lax.erf(pre * 0.7071067811865476))
            pdf = jnp.exp(-0.5 * pre * pre) * 0.3989422804014327
            act = (pre * cdf).astype(jnp.bfloat16)
            ga = jnp.dot(w2t_ref[ks, :], ub, preferred_element_type=f32)
            gp = (ga * (cdf + pre * pdf)).astype(jnp.bfloat16)
            gs_ref[ks, :] += lax.dot_general(act, ub, across, preferred_element_type=f32)
            gf_ref[ks, :] += lax.dot_general(gp, mb, across, preferred_element_type=f32)
            part = jnp.dot(w1t_ref[:, ks], gp, preferred_element_type=f32)
            total = part if total is None else total + part
        gmix[b] = total
        return 0

    lax.fori_loop(0, images, image, 0)

    lane = lax.broadcasted_iota(jnp.int32, (images, width), 1)

    def finish(first, count, mean, inv, carry, tile):
        s1, s2, ga, sh = carry
        for j in range(count):
            t = tile[j]
            gm_ref[first + j] = t.astype(jnp.bfloat16)
            x = x_ref[first + j].astype(f32)
            normed = (x - mean[:, j : j + 1]) * inv[:, j : j + 1]
            tn = t * normed
            ga = ga + tn
            sh = sh + t
            s1 = column(lane, first + j, jnp.sum(t * gain, axis=-1, keepdims=True), s1)
            s2 = column(lane, first + j, jnp.sum(tn * gain, axis=-1, keepdims=True), s2)
        return s1, s2, ga, sh

    def post(i, carry):
        first = pl.multiple_of(i * T, T)
        tile = jnp.swapaxes(gmix[:, pl.ds(first, T), :], 0, 1)
        return finish(first, T, rolled(i, 0), rolled(i, 1), carry, tile)

    zs = jnp.zeros((images, width), f32)
    zc = jnp.zeros((images, chans), f32)
    carry = lax.fori_loop(0, full, post, (zs, zs, zc, zc))
    if tail:
        tile = jnp.swapaxes(gmix[:, start:padded, :], 0, 1)
        carry = finish(
            start, tail, stat_ref[0, :, start:], stat_ref[1, :, start:], carry, tile
        )
    s1, s2, ga, sh = carry
    sums_ref[0] = s1
    sums_ref[1] = s2
    chan_ref[0:1, :] += jnp.sum(ga, axis=0, keepdims=True)
    chan_ref[1:2, :] += jnp.sum(sh, axis=0, keepdims=True)


def final_kernel(x_ref, up_ref, gm_ref, stat_ref, sums_ref, gain_ref, out_ref):
    i = pl.program_id(0)
    width = stat_ref.shape[2]
    gain = gain_ref[...]
    shift = lax.rem(width - i * T, width)
    mean, inv = pltpu.roll(stat_ref[0], shift, 1), pltpu.roll(stat_ref[1], shift, 1)
    s1, s2 = pltpu.roll(sums_ref[0], shift, 1), pltpu.roll(sums_ref[1], shift, 1)
    for j in range(T):
        c = slice(j, j + 1)
        x = x_ref[j].astype(jnp.float32)
        normed = (x - mean[:, c]) * inv[:, c]
        inner = gm_ref[j].astype(jnp.float32) * gain - s1[:, c] - normed * s2[:, c]
        out_ref[j] = (up_ref[j].astype(jnp.float32) + inv[:, c] * inner).astype(jnp.bfloat16)


def others(x, axis):
    n = lax.axis_size(axis)
    return [x] + [
        lax.ppermute(x, axis, [(i, (i + s) % n) for i in range(n)]) for s in range(1, n)
    ]


def per_device(inputs, norm_gain, norm_bias, w_first, b_first, w_second, upstream):
    f32 = jnp.float32
    batch, patches, chans = inputs.shape
    hidden = w_first.shape[0]
    n_chan, n_dp = lax.axis_size("chan"), lax.axis_size("dp")
    width = chans * n_chan
    scale = 1.0 / (batch * n_dp)
    padded = -(-(patches + 3) // T) * T
    x = jnp.transpose(inputs, (1, 0, 2))
    up = jnp.transpose(upstream, (1, 0, 2))
    steps = -(-patches // T)
    S = jax.ShapeDtypeStruct
    params = functools.partial(pltpu.CompilerParams, dimension_semantics=("arbitrary",))

    local = pl.pallas_call(
        stats_kernel,
        grid=(steps,),
        in_specs=[pl.BlockSpec((T, batch, chans), lambda i: (i, 0, 0))],
        out_specs=pl.BlockSpec((2, batch, LANES), lambda i: (0, 0, 0)),
        out_shape=S((2, batch, LANES), f32),
        compiler_params=params(),
    )(x)
    every = others(local, "chan")
    mean = sum(e[0] for e in every) / n_chan
    squares = sum(e[1] for e in every) + chans * sum(
        (e[0] - mean) * (e[0] - mean) for e in every
    )
    stat = jnp.stack([mean, lax.rsqrt(squares / width + epsilon)])

    high = lax.reduce_precision(b_first, 8, 7)
    middle = lax.reduce_precision(b_first - high, 8, 7)
    low = b_first - high - middle
    extra = jnp.stack([high, middle, low], axis=1).astype(jnp.bfloat16)
    w1 = jnp.concatenate([w_first, extra], axis=1)
    w1 = jnp.pad(w1, ((0, 0), (0, padded - patches - 3)))
    w1t = jnp.pad(w_first.T, ((0, padded - patches), (0, 0)))
    w2t = jnp.pad(w_second.T, ((0, 0), (0, padded - patches)))
    gain2, bias2 = norm_gain[None, :], norm_bias[None, :]

    whole = lambda shape: pl.BlockSpec(shape, lambda g: (0,) * len(shape))
    group = T
    big = pl.BlockSpec((patches, group, chans), lambda g: (0, g, 0))
    pair = pl.BlockSpec((2, group, LANES), lambda g: (0, g, 0))
    gm, sums, gf, gs, chan = pl.pallas_call(
        functools.partial(main_kernel, patches),
        grid=(batch // group,),
        in_specs=[
            big,
            big,
            pair,
            whole((1, chans)),
            whole((1, chans)),
            whole((hidden, padded)),
            whole((padded, hidden)),
            whole((hidden, padded)),
        ],
        out_specs=[big, pair, whole((hidden, padded)), whole((hidden, padded)), whole((2, chans))],
        out_shape=[
            S((patches, batch, chans), jnp.bfloat16),
            S((2, batch, LANES), f32),
            S((hidden, padded), f32),
            S((hidden, padded), f32),
            S((2, chans), f32),
        ],
        scratch_shapes=[
            pltpu.VMEM((group, padded, chans), jnp.bfloat16),
            pltpu.VMEM((group, padded, chans), jnp.bfloat16),
            pltpu.VMEM((group, padded, chans), f32),
        ],
        compiler_params=params(vmem_limit_bytes=56 * MIB),
    )(x, up, stat, gain2, bias2, w1, w1t, w2t)

    flat = jnp.pad(chan.reshape(-1), (0, -(2 * chans) % hidden)).reshape(hidden, -1)
    packed = jnp.concatenate([gf[:, : patches + 1], gs[:, :patches], flat], axis=1)
    owned = lax.psum_scatter(packed, "dp", scatter_dimension=0, tiled=True)
    sums = sum(others(sums, "chan")) / width

    pblock = pl.BlockSpec((T, batch, chans), lambda i: (i, 0, 0))
    out = pl.pallas_call(
        final_kernel,
        grid=(steps,),
        in_specs=[
            pblock,
            pblock,
            pblock,
            whole((2, batch, LANES)),
            whole((2, batch, LANES)),
            whole((1, chans)),
        ],
        out_specs=pblock,
        out_shape=S((patches, batch, chans), jnp.bfloat16),
        compiler_params=params(),
        cost_estimate=pl.CostEstimate(
            flops=12 * x.size, bytes_accessed=8 * x.size, transcendentals=0
        ),
    )(x, up, gm, stat, sums, gain2)

    cut = 2 * patches + 1
    chan = lax.all_gather(owned[:, cut:], "dp", tiled=True)
    chan = chan.reshape(-1)[: 2 * chans].reshape(2, chans) * scale
    mine = sum(others(owned[:, :cut], "chan")) * scale
    return (
        jnp.transpose(out, (1, 0, 2)),
        mine[:, :patches],
        mine[:, patches + 1 :].T,
        mine[:, patches],
        chan[0],
        chan[1],
    )


def solution(mesh):
    in_specs = (P("dp", None, "chan"), P("chan"), P("chan"), P(), P(), P(), P("dp", None, "chan"))
    out_specs = (P("dp", None, "chan"), P("dp", None), P(None, "dp"), P("dp"), P("chan"), P("chan"))
    return jax.shard_map(
        per_device, mesh=mesh, in_specs=in_specs, out_specs=out_specs, check_vma=False
    )
```

profile of v0, /device:TPU:0, one launch (start us, length us, event | category | flops | bytes accessed | tf_op | source)
XLA Modules:
  0.0 236.9 jit_solution(8619806388326874302)
XLA Ops:
  7.2 0.0 reduce-scatter.2.cloned.1.call-start
  7.2 13.3 %shard_map.118 = f32[2,48,256]{2,1,0:T(8,128)} custom-call(bf16[196,48,512]{2,1,0:T(8,128)(2,1)} %bitcast.13), custom_call_target="tpu_custom_call" | custom-call | tf_op jit(solution)/shard_map/pallas_call | solution.py:203
  20.5 3.0 %collective-permute-start = (f32[2,48,256]{2,1,0:T(8,128)}, f32[2,48,256]{2,1,0:T(8,128)S(1)}, u32[]{:S(2)}, u32[]{:S(2)}) collective-permute-start(f32[2,48,256]{2,1,0:T(8,128)} %shard_map.118), channel_id=1, source_target_pairs={{0,1},{1,0},{2,3},{3,2},{4,5},{5,4},{6,7},{7,6},{8,9},{9,8},{10,11... | collective-permute-start | bytes 294920 | tf_op jit(solution)/shard_map/ppermute | solution.py:185
  23.5 0.1 stack.23
  23.6 0.1 stack.24
  23.8 0.1 stack.25
  23.9 0.1 copy.24
  24.1 0.1 copy.28
  24.2 0.7 pad.14.w2t_ref
  25.0 0.7 pad.13.w1t_ref
  25.7 0.9 fusion.6.w1_ref
  26.6 0.9 fusion.10
  27.4 0.7 pad_maximum_fusion.1.stat_ref
  28.1 113.5 %shard_map.119 = (bf16[196,48,512]{2,1,0:T(8,128)(2,1)}, f32[2,48,256]{2,1,0:T(8,128)}, f32[512,208]{1,0:T(8,128)}, f32[512,208]{1,0:T(8,128)}, f32[2,512]{1,0:T(2,128)}) custom-call(bf16[196,48,512]{2,1,0:T(8,128)(2,1)} %bitcast.14, bf16[196,48,512]{2,1,0:T(8,128)(2,1)} %bitcast.16, f32[2,48,256]{2,1,0:T(8,128)} %pad_maximum_fusion.1.stat_ref, ...), custom_call_target="tpu_custom_call" | custom-call | tf_op jit(solution)/shard_map/pallas_call | solution.py:232
  141.6 0.9 reshape.23
  142.5 2.5 %pad_maximum_fusion = f32[512,395]{1,0:T(8,128)} fusion(f32[512,2]{1,0:T(8,128)S(1)} %reshape.23, f32[512,196]{1,0:T(8,128)} %bitcast.22, f32[512,197]{1,0:T(8,128)} %bitcast.21), kind=kLoop, calls=%fused_computation | loop fusion | flops 404480 | bytes 1617920 | tf_op jit(solution)/shard_map/concatenate | solution.py:262
  145.0 1.8 collective-permute-start.1
  146.9 3.1 %collective-permute-done.1 = f32[2,48,256]{2,1,0:T(8,128)S(1)} collective-permute-done((f32[2,48,256]{2,1,0:T(8,128)}, f32[2,48,256]{2,1,0:T(8,128)S(1)}, u32[]{:S(2)}, u32[]{:S(2)}) %collective-permute-start.1) | collective-permute-done | bytes 98336 | tf_op jit(solution)/shard_map/ppermute | solution.py:185
  149.9 1.5 add_multiply_fusion.sums_ref
  151.5 20.1 %shard_map.120 = bf16[196,48,512]{2,1,0:T(8,128)(2,1)} custom-call(bf16[196,48,512]{2,1,0:T(8,128)(2,1)} %bitcast.15, bf16[196,48,512]{2,1,0:T(8,128)(2,1)} %bitcast.17, bf16[196,48,512]{2,1,0:T(8,128)(2,1)} %get-tuple-element.11.gm_ref, f32[2,48,256]{2,1,0:T(8,128)} %pad_maximum_fusion.1.stat_ref, f32[2,48,256]{2,1,0:T(8,128)} %add_multiply_fusion.sums_ref, ...), custom_call_target="tpu_custom_call" | custom-call | flops 57802752 | bytes 38535168 | tf_op jit(solution)/shard_map/pallas_call | solution.py:267
  171.6 32.6 %reduce-scatter.2.cloned.1.call-done = f32[32,395]{1,0:T(8,128)} async-done(((f32[512,395]{1,0:T(8,128)}), f32[32,395]{1,0:T(8,128)}) %reduce-scatter.2.cloned.1.call-update) | async-done | bytes 50576 | tf_op jit(solution)/shard_map/reduce_scatter | solution.py:263
  204.2 1.5 collective-permute-start.2
  205.7 0.8 slice.68
  206.6 0.1 copy.29
  206.6 19.4 %all-gather = f32[16,32,2]{1,2,0:T(2,128)S(1)} all-gather(f32[1,32,2]{1,2,0:T(2,128)S(1)} %bitcast.26), channel_id=1, replica_groups=mesh['dp'=16,'chan'=2] {'dp'}, dimensions={0}, use_global_device_ids=true | all-gather | bytes 4352 | tf_op jit(solution)/shard_map/all_gather | solution.py:287
  226.1 0.1 copy.30
  226.2 0.7 squeeze.7
  226.9 0.1 copy.31
  227.1 0.7 squeeze.8
  227.8 0.9 add_multiply_fusion.1
  228.6 0.7 slice_bitcast_fusion
  229.3 0.7 slice_reduce_fusion
  (12 shorter events, 0.1 us)
Async XLA Ops:
  7.2 16.3 %copy-start.2 = (f32[512]{0:T(512)S(1)}, f32[512]{0:T(512)}, u32[]{:S(2)}) copy-start(f32[512]{0:T(512)} %param.11) | copy-start | bytes 6148
  7.2 16.8 %copy-start = (bf16[512,196]{0,1:T(8,128)(2,1)S(1)}, bf16[512,196]{0,1:T(8,128)(2,1)}, u32[]{:S(2)}) copy-start(bf16[512,196]{0,1:T(8,128)(2,1)} %param.10) | copy-start | bytes 602116
  7.2 16.9 %copy-start.1 = (bf16[196,512]{1,0:T(8,128)(2,1)S(1)}, bf16[196,512]{1,0:T(8,128)(2,1)}, u32[]{:S(2)}) copy-start(bf16[196,512]{1,0:T(8,128)(2,1)} %param.12) | copy-start | bytes 602116
  7.2 197.0 %reduce-scatter.2.cloned.1.call-start = ((), (), s32[]{:S(2)}) async-start(), calls=%async_computation.1 | async-start | bytes 1114112 | tf_op jit(solution)/shard_map/reduce_scatter | solution.py:263
  20.5 6.0 %collective-permute-start = (f32[2,48,256]{2,1,0:T(8,128)}, f32[2,48,256]{2,1,0:T(8,128)S(1)}, u32[]{:S(2)}, u32[]{:S(2)}) collective-permute-start(f32[2,48,256]{2,1,0:T(8,128)} %shard_map.118), channel_id=1, source_target_pairs={{0,1},{1,0},{2,3},{3,2},{4,5},{5,4},{6,7},{7,6},{8,9},{9,8},{10,11... | collective-permute-start | bytes 294920 | tf_op jit(solution)/shard_map/ppermute | solution.py:185
  145.0 4.9 %collective-permute-start.1 = (f32[2,48,256]{2,1,0:T(8,128)}, f32[2,48,256]{2,1,0:T(8,128)S(1)}, u32[]{:S(2)}, u32[]{:S(2)}) collective-permute-start(f32[2,48,256]{2,1,0:T(8,128)} %get-tuple-element.12), channel_id=1, source_target_pairs={{0,1},{1,0},{2,3},{3,2},{4,5},{5,4},{6,7},{7,6},{8,9},{9,8},{10,11... | collective-permute-start | bytes 294920 | tf_op jit(solution)/shard_map/ppermute | solution.py:185
  204.2 23.5 %collective-permute-start.2 = (f32[32,393]{1,0:T(8,128)}, f32[32,393]{1,0:T(8,128)S(1)}, u32[]{:S(2)}, u32[]{:S(2)}) collective-permute-start(f32[32,393]{1,0:T(8,128)} %bitcast.23), channel_id=1, source_target_pairs={{0,1},{1,0},{2,3},{3,2},{4,5},{5,4},{6,7},{7,6},{8,9},{9,8},{10,11... | collective-permute-start | bytes 150920 | tf_op jit(solution)/shard_map/ppermute | solution.py:185
Sparse Core Ops, SparseCore 0:
  145.2 59.0 reduce-scatter.1
where the time goes:
time: 238 us; the launch traced here: 237 us
  Pallas kernels  147 us (62%)
  waiting for transfers between devices  35.7 us (15%)
  blocking collectives  19.4 us (8%)
  between operations  14.1 us (6%)
  other arithmetic  7.38 us (3%)
  local copies, waits for them, and re-layouts  7 us (3%)
  starting transfers between devices  6.3 us (3%)
    pallas_call x1, Pallas kernels, per_device(): pl.pallas_call(functools.partial(main_kernel, patches), grid=(batch // gr...  113 us
    reduce_scatter x1, waiting for transfers between devices, per_device(): owned = lax.psum_scatter(packed, 'dp', scatter_dimension=0, tiled=True)  32.6 us
    pallas_call x1, Pallas kernels, per_device(): pl.pallas_call(final_kernel, grid=(steps,), in_specs=[pblock, pblock, pbl...  20.1 us
    all_gather x1, blocking collectives, per_device(): chan = lax.all_gather(owned[:, cut:], 'dp', tiled=True)  19.4 us
    pallas_call x1, Pallas kernels, per_device(): pl.pallas_call(stats_kernel, grid=(steps,), in_specs=[pl.BlockSpec((T, ba...  13.3 us
    ppermute x3, starting transfers between devices, others(): lax.ppermute(x, axis, [(i, (i + s) % n) for i in range(n)])  6.26 us
  transfers between devices with their start and end apart: 4, of which 2 were waited for; matrix products, arithmetic and copies ran while one was open for 3% of the time, Pallas kernels for 9%

commit v1 on v0

v1 whole, which is shorter than its diff:
```python
import functools

import jax
import jax.numpy as jnp
from jax import lax
from jax.experimental import pallas as pl
from jax.experimental.pallas import tpu as pltpu
from jax.sharding import PartitionSpec as P

epsilon = 1e-06
T = 16
LANES = 256
MIB = 2**20


def column(lane, p, value, held):
    return jnp.where(lane == p, value, held)


def stats_kernel(x_ref, out_ref):
    i = pl.program_id(0)
    chans = x_ref.shape[2]
    images = x_ref.shape[1]
    lane = lax.broadcasted_iota(jnp.int32, (images, out_ref.shape[2]), 1)

    @pl.when(i == 0)
    def _():
        out_ref[...] = jnp.zeros_like(out_ref)

    means, squares = out_ref[0], out_ref[1]
    rows = x_ref.shape[0]
    for j in range(rows):
        x = x_ref[j].astype(jnp.float32)
        mean = jnp.sum(x, axis=-1, keepdims=True) * (1.0 / chans)
        d = x - mean
        square = jnp.sum(d * d, axis=-1, keepdims=True)
        means = column(lane, i * rows + j, mean, means)
        squares = column(lane, i * rows + j, square, squares)
    out_ref[0] = means
    out_ref[1] = squares


def main_kernel(
    patches,
    x_ref,
    up_ref,
    stat_ref,
    gain_ref,
    bias_ref,
    w1_ref,
    w1t_ref,
    w2t_ref,
    w1f_ref,
    vec_ref,
    gm_ref,
    sums_ref,
    gf_ref,
    gs_ref,
    mixed,
    upper,
    gmix,
):
    g = pl.program_id(0)
    images, width = stat_ref.shape[1], stat_ref.shape[2]
    chans = x_ref.shape[2]
    hidden = w1_ref.shape[0]
    padded = w1_ref.shape[1]
    full, tail = patches // T, patches % T
    f32 = jnp.float32

    @pl.when(g == 0)
    def _():
        gf_ref[...] = jnp.zeros_like(gf_ref)
        gs_ref[...] = jnp.zeros_like(gs_ref)

    gain = gain_ref[...]
    bias = bias_ref[...]

    def prepare(first, count, mean, inv):
        rows = []
        for j in range(count):
            x = x_ref[first + j].astype(f32)
            normed = (x - mean[:, j : j + 1]) * inv[:, j : j + 1]
            rows.append((normed * gain + bias).astype(jnp.bfloat16))
        return rows

    def rolled(i, which):
        return pltpu.roll(stat_ref[which], lax.rem(width - i * T, width), 1)

    def step(i, _):
        first = pl.multiple_of(i * T, T)
        rows = prepare(first, T, rolled(i, 0), rolled(i, 1))
        mixed[:, pl.ds(first, T), :] = jnp.swapaxes(jnp.stack(rows), 0, 1)
        upper[:, pl.ds(first, T), :] = jnp.swapaxes(up_ref[pl.ds(first, T)], 0, 1)
        return 0

    lax.fori_loop(0, full, step, 0)
    start = full * T
    one = jnp.ones((images, chans), jnp.bfloat16)
    zero = jnp.zeros((images, chans), jnp.bfloat16)
    rows = prepare(start, tail, stat_ref[0, :, start:], stat_ref[1, :, start:]) + [one] * 3
    rows = rows + [zero] * (padded - start - len(rows))
    mixed[:, start:padded, :] = jnp.swapaxes(jnp.stack(rows), 0, 1)
    ups = [up_ref[start + j] for j in range(tail)]
    ups = ups + [zero] * (padded - start - tail)
    upper[:, start:padded, :] = jnp.swapaxes(jnp.stack(ups), 0, 1)

    block = 256
    across = (((1,), (1,)), ((), ()))

    def image(b, _):
        mb = mixed[b]
        ub = upper[b]
        total = None
        second = jnp.zeros((8, padded), f32)
        for k in range(0, hidden, block):
            ks = slice(k, k + block)
            pre = jnp.dot(w1_ref[ks, :], mb, preferred_element_type=f32)
            ga = jnp.dot(w2t_ref[ks, :], ub, preferred_element_type=f32)
            u = pre * 0.7071067811865476
            twice = 1.0 + lax.erf(u)
            slope = (u * 1.1283791670955126) * jnp.exp2(u * u * -1.4426950408889634)
            act = (pre * twice).astype(jnp.bfloat16)
            gp = (ga * (twice + slope)).astype(jnp.bfloat16)
            gs_ref[ks, :] += lax.dot_general(act, ub, across, preferred_element_type=f32)
            gf = lax.dot_general(gp, mb, across, preferred_element_type=f32)
            gf_ref[ks, :] += gf
            second = second + jnp.sum((gf * w1f_ref[ks, :]).reshape(-1, 8, padded), axis=0)
            part = jnp.dot(w1t_ref[:, ks], gp, preferred_element_type=f32)
            total = part if total is None else total + part
        rounded = total.astype(jnp.bfloat16)
        gmix[b] = rounded
        dots = lax.dot_general(vec_ref[...], rounded, across, preferred_element_type=f32)
        second = jnp.sum(second, axis=0, keepdims=True)
        sums_ref[0, pl.ds(b, 1), :padded] = dots[0:1] + dots[1:2]
        sums_ref[1, pl.ds(b, 1), :padded] = second - (dots[2:3] + dots[3:4])
        return 0

    lax.fori_loop(0, images, image, 0)

    def post(i, _):
        first = pl.multiple_of(i * T, T)
        gm_ref[pl.ds(first, T)] = jnp.swapaxes(gmix[:, pl.ds(first, T), :], 0, 1)
        return 0

    lax.fori_loop(0, full, post, 0)
    if tail:
        tile = jnp.swapaxes(gmix[:, start:padded, :], 0, 1)
        gm_ref[start:] = tile[:tail]


def final_kernel(x_ref, up_ref, gm_ref, stat_ref, sums_ref, gain_ref, out_ref, chan_ref):
    i = pl.program_id(0)
    rows = x_ref.shape[0]
    width = stat_ref.shape[2]
    gain = gain_ref[...]

    @pl.when(i == 0)
    def _():
        chan_ref[...] = jnp.zeros_like(chan_ref)

    shift = lax.rem(width - i * rows, width)
    mean, inv = pltpu.roll(stat_ref[0], shift, 1), pltpu.roll(stat_ref[1], shift, 1)
    s1, s2 = pltpu.roll(sums_ref[0], shift, 1), pltpu.roll(sums_ref[1], shift, 1)
    products = jnp.zeros(x_ref.shape[1:], jnp.float32)
    plain = jnp.zeros(x_ref.shape[1:], jnp.float32)
    for j in range(rows):
        c = slice(j, j + 1)
        x = x_ref[j].astype(jnp.float32)
        normed = (x - mean[:, c]) * inv[:, c]
        t = gm_ref[j].astype(jnp.float32)
        products = products + t * normed
        plain = plain + t
        inner = t * gain - s1[:, c] - normed * s2[:, c]
        out_ref[j] = (up_ref[j].astype(jnp.float32) + inv[:, c] * inner).astype(jnp.bfloat16)
    chan_ref[0:1, :] += jnp.sum(products, axis=0, keepdims=True)
    chan_ref[1:2, :] += jnp.sum(plain, axis=0, keepdims=True)


def reduce_kernel(scale, first_ref, second_ref, chan_ref, out_ref, chan_out_ref, *scratch):
    one, one_c, held, held_c, two, two_c, own, three, sems, sems2, sems3 = scratch
    me, col = lax.axis_index("dp"), lax.axis_index("chan")
    n_dp, n_chan = lax.axis_size("dp"), lax.axis_size("chan")
    halves = n_dp // 2
    mine, core = me // 2, me % 2
    partner = me + 1 - 2 * core
    peers = [((mine + j) % halves) * 2 + core for j in range(1, halves)]
    columns = [(col + s) % n_chan for s in range(1, n_chan)]
    mesh_id = pl.DeviceIdType.MESH

    barrier = pltpu.get_barrier_semaphore()
    for d in [partner] + peers:
        pl.semaphore_signal(barrier, inc=1, device_id=(d, col), device_id_type=mesh_id)
    for d in columns:
        pl.semaphore_signal(barrier, inc=1, device_id=(me, d), device_id_type=mesh_id)
    pl.semaphore_wait(barrier, halves + n_chan - 1)

    def send(src, dst, sem, k, target):
        copy = pltpu.make_async_remote_copy(
            src_ref=src,
            dst_ref=dst,
            send_sem=sem.at[0, k],
            recv_sem=sem.at[1, k],
            device_id=target,
            device_id_type=mesh_id,
        )
        copy.start()
        return copy

    copies = [
        send(first_ref.at[:, 1 - core], one.at[0], sems, 0, (partner, col)),
        send(second_ref.at[:, 1 - core], one.at[1], sems, 1, (partner, col)),
        send(chan_ref, one_c, sems, 2, (partner, col)),
    ]
    for c in copies:
        c.wait()

    def add(t, _):
        held[t, 0] = first_ref[t, core] + one[0, t]
        held[t, 1] = second_ref[t, core] + one[1, t]
        return 0

    lax.fori_loop(0, halves, add, 0)
    held_c[...] = chan_ref[...] + one_c[...]
    copies = []
    for j in range(1, halves):
        t = (mine + j) % halves
        copies.append(send(held.at[t], two.at[j - 1], sems2, 2 * j - 2, (2 * t + core, col)))
        copies.append(send(held_c, two_c.at[mine], sems2, 2 * j - 1, (2 * t + core, col)))
    two_c[mine] = held_c[...]
    for c in copies:
        c.wait()
    total = held[mine]
    for j in range(1, halves):
        total = total + two[j - 1]
    own[...] = total
    copies = [
        send(own, three.at[col], sems3, s, (me, d)) for s, d in enumerate(columns)
    ]
    three[col] = total
    chan_sum = two_c[0]
    for j in range(1, halves):
        chan_sum = chan_sum + two_c[j]
    chan_out_ref[...] = chan_sum * scale
    for c in copies:
        c.wait()
    total = three[0]
    for j in range(1, n_chan):
        total = total + three[j]
    out_ref[...] = total * scale


def reduce_all(first, second, chan, scale):
    n_dp, n_chan = lax.axis_size("dp"), lax.axis_size("chan")
    halves = n_dp // 2
    rows, lanes = first.shape[0] // n_dp, first.shape[1]
    f32 = jnp.float32
    S = jax.ShapeDtypeStruct
    vmem = pl.BlockSpec(memory_space=pltpu.VMEM)
    shape = (halves, 2, rows, lanes)
    dma = pltpu.SemaphoreType.DMA
    return pl.pallas_call(
        functools.partial(reduce_kernel, scale),
        in_specs=[vmem] * 3,
        out_specs=[vmem] * 2,
        out_shape=[S((2, rows, lanes), f32), S(chan.shape, f32)],
        scratch_shapes=[
            pltpu.VMEM((2, halves, rows, lanes), f32),
            pltpu.VMEM(chan.shape, f32),
            pltpu.VMEM(shape, f32),
            pltpu.VMEM(chan.shape, f32),
            pltpu.VMEM((halves - 1, 2, rows, lanes), f32),
            pltpu.VMEM((halves,) + chan.shape, f32),
            pltpu.VMEM((2, rows, lanes), f32),
            pltpu.VMEM((n_chan, 2, rows, lanes), f32),
            dma((2, 3)),
            dma((2, 2 * halves - 2)),
            dma((2, n_chan - 1)),
        ],
        compiler_params=pltpu.CompilerParams(collective_id=0, has_side_effects=True),
    )(first.reshape(shape), second.reshape(shape), chan)


def others(x, axis):
    n = lax.axis_size(axis)
    return [x] + [
        lax.ppermute(x, axis, [(i, (i + s) % n) for i in range(n)]) for s in range(1, n)
    ]


def per_device(inputs, norm_gain, norm_bias, w_first, b_first, w_second, upstream):
    f32 = jnp.float32
    batch, patches, chans = inputs.shape
    hidden = w_first.shape[0]
    n_chan, n_dp = lax.axis_size("chan"), lax.axis_size("dp")
    width = chans * n_chan
    scale = 1.0 / (batch * n_dp)
    padded = -(-(patches + 3) // T) * T
    x = jnp.transpose(inputs, (1, 0, 2))
    up = jnp.transpose(upstream, (1, 0, 2))
    rows = max(r for r in range(1, T + 1) if patches % r == 0)
    steps = patches // rows
    S = jax.ShapeDtypeStruct
    params = functools.partial(pltpu.CompilerParams, dimension_semantics=("arbitrary",))

    local = pl.pallas_call(
        stats_kernel,
        grid=(steps,),
        in_specs=[pl.BlockSpec((rows, batch, chans), lambda i: (i, 0, 0))],
        out_specs=pl.BlockSpec((2, batch, LANES), lambda i: (0, 0, 0)),
        out_shape=S((2, batch, LANES), f32),
        compiler_params=params(),
    )(x)
    every = others(local, "chan")
    mean = sum(e[0] for e in every) / n_chan
    squares = sum(e[1] for e in every) + chans * sum(
        (e[0] - mean) * (e[0] - mean) for e in every
    )
    stat = jnp.stack([mean, lax.rsqrt(squares / width + epsilon)])

    high = lax.reduce_precision(b_first, 8, 7)
    middle = lax.reduce_precision(b_first - high, 8, 7)
    low = b_first - high - middle
    extra = jnp.stack([high, middle, low], axis=1).astype(jnp.bfloat16)
    w1 = jnp.concatenate([w_first, extra], axis=1)
    w1 = jnp.pad(w1, ((0, 0), (0, padded - patches - 3)))
    w1t = jnp.pad(w_first.T, ((0, padded - patches), (0, 0)))
    w2t = jnp.pad(0.5 * w_second.T, ((0, 0), (0, padded - patches)))
    w1f = w1t.T.astype(f32)
    gain2, bias2 = norm_gain[None, :], norm_bias[None, :]
    lead = lax.reduce_precision(jnp.stack([norm_gain, norm_bias]), 8, 7)
    rest = jnp.stack([norm_gain, norm_bias]) - lead
    vec = jnp.stack([lead[0], rest[0], lead[1], rest[1]]).astype(jnp.bfloat16)
    vec = jnp.pad(vec, ((0, T - 4), (0, 0)))

    whole = lambda shape: pl.BlockSpec(shape, lambda g: (0,) * len(shape))
    group = T
    big = pl.BlockSpec((patches, group, chans), lambda g: (0, g, 0))
    pair = pl.BlockSpec((2, group, LANES), lambda g: (0, g, 0))
    gm, sums, gf, gs = pl.pallas_call(
        functools.partial(main_kernel, patches),
        grid=(batch // group,),
        in_specs=[
            big,
            big,
            pair,
            whole((1, chans)),
            whole((1, chans)),
            whole((hidden, padded)),
            whole((padded, hidden)),
            whole((hidden, padded)),
            whole((hidden, padded)),
            whole((T, chans)),
        ],
        out_specs=[big, pair, whole((hidden, padded)), whole((hidden, padded))],
        out_shape=[
            S((patches, batch, chans), jnp.bfloat16),
            S((2, batch, LANES), f32),
            S((hidden, padded), f32),
            S((hidden, padded), f32),
        ],
        scratch_shapes=[
            pltpu.VMEM((group, padded, chans), jnp.bfloat16),
            pltpu.VMEM((group, padded, chans), jnp.bfloat16),
            pltpu.VMEM((group, padded, chans), jnp.bfloat16),
        ],
        compiler_params=params(vmem_limit_bytes=56 * MIB),
    )(x, up, stat, gain2, bias2, w1, w1t, w2t, w1f, vec)

    sums = sum(others(sums, "chan")) / width

    pblock = pl.BlockSpec((rows, batch, chans), lambda i: (i, 0, 0))
    out, chan = pl.pallas_call(
        final_kernel,
        grid=(steps,),
        in_specs=[
            pblock,
            pblock,
            pblock,
            whole((2, batch, LANES)),
            whole((2, batch, LANES)),
            whole((1, chans)),
        ],
        out_specs=[pblock, whole((2, chans))],
        out_shape=[S((patches, batch, chans), jnp.bfloat16), S((2, chans), f32)],
        compiler_params=params(),
        cost_estimate=pl.CostEstimate(
            flops=12 * x.size, bytes_accessed=8 * x.size, transcendentals=0
        ),
    )(x, up, gm, stat, sums, gain2)

    mine, chan = reduce_all(gf, gs, chan, scale)
    return (
        jnp.transpose(out, (1, 0, 2)),
        mine[0, :, :patches],
        (0.5 * mine[1, :, :patches]).T,
        mine[0, :, patches],
        chan[0],
        chan[1],
    )


def solution(mesh):
    in_specs = (P("dp", None, "chan"), P("chan"), P("chan"), P(), P(), P(), P("dp", None, "chan"))
    out_specs = (P("dp", None, "chan"), P("dp", None), P(None, "dp"), P("dp"), P("chan"), P("chan"))
    return jax.shard_map(
        per_device, mesh=mesh, in_specs=in_specs, out_specs=out_specs, check_vma=False
    )
```

time: 238 us -> 160 us (0.67)
  waiting for transfers between devices: 35.7 us -> 4.74 us
  blocking collectives: 19.4 us -> 0 us
  between operations: 14.1 us -> 0.77 us
  Pallas kernels: 147 us -> 137 us
  starting transfers between devices: 6.3 us -> 3.12 us
    reduce_scatter x1 -> x0, waiting for transfers between devices: 32.6 us -> none  [per_device(): owned = lax.psum_scatter(packed, 'dp', scatter_dimension=0, tiled=True)]
    pallas_call x1, Pallas kernels: 113 us -> 82.9 us  [per_device(): pl.pallas_call(functools.partial(main_kernel, patches), grid=(batch // gr...]
    pallas_call x1 -> x2, Pallas kernels: 13.3 us -> 33.4 us  [the longest x1 20.9 us: reduce_all(): pl.pallas_call(functools.partial(reduce_kernel, scale), in_specs=[vmem] *...]
    all_gather x1 -> x0, blocking collectives: 19.4 us -> none  [per_device(): chan = lax.all_gather(owned[:, cut:], 'dp', tiled=True)]
    ppermute x3 -> x2, starting transfers between devices: 6.26 us -> 3.12 us  [others(): lax.ppermute(x, axis, [(i, (i + s) % n) for i in range(n)])]
    concatenate x1 -> x0, other arithmetic: 2.55 us -> none  [per_device(): jnp.concatenate([gf[:, :patches + 1], gs[:, :patches], flat], axis=1)]
  transfers between devices with their start and end apart: 4 -> 2, of which waited for: 2 -> 1; matrix products, arithmetic and copies ran while one was open for 3% -> 3% of each run, Pallas kernels for 9% -> 0%
where the time goes in v1:
time: 160 us; the launch traced here: 158 us
  Pallas kernels  137 us (86%)
  other arithmetic  6.87 us (4%)
  local copies, waits for them, and re-layouts  5 us (3%)
  waiting for transfers between devices  4.74 us (3%)
  starting transfers between devices  3.12 us (2%)
    pallas_call x1, Pallas kernels, per_device(): pl.pallas_call(functools.partial(main_kernel, patches), grid=(batch // gr...  82.9 us
    pallas_call x1, Pallas kernels, reduce_all(): pl.pallas_call(functools.partial(reduce_kernel, scale), in_specs=[vmem] *...  20.9 us
    pallas_call x1, Pallas kernels, per_device(): pl.pallas_call(final_kernel, grid=(steps,), in_specs=[pblock, pblock, pbl...  20.9 us
    pallas_call x1, Pallas kernels, per_device(): pl.pallas_call(stats_kernel, grid=(steps,), in_specs=[pl.BlockSpec((rows,...  12.5 us
    ppermute x2, waiting for transfers between devices, others(): lax.ppermute(x, axis, [(i, (i + s) % n) for i in range(n)])  4.74 us
  transfers between devices with their start and end apart: 2, of which 1 were waited for; matrix products, arithmetic and copies ran while one was open for 3% of the time, Pallas kernels for 0%

profile of v1, /device:TPU:0, one launch (start us, length us, event | category | flops | bytes accessed | tf_op | source)
XLA Modules:
  0.0 157.6 jit_solution(15327298417425978418)
XLA Ops:
  0.6 0.0 copy-start
  0.6 0.0 copy-start.4
  0.7 0.0 copy-start.1
  0.7 0.0 copy-start.3
  0.7 0.0 copy-start.2
  0.7 12.5 %shard_map.118 = f32[2,48,256]{2,1,0:T(8,128)} custom-call(bf16[196,48,512]{2,1,0:T(8,128)(2,1)} %bitcast.20), custom_call_target="tpu_custom_call" | custom-call | tf_op jit(solution)/shard_map/pallas_call | solution.py:306
  13.2 3.0 %collective-permute-start = (f32[2,48,256]{2,1,0:T(8,128)}, f32[2,48,256]{2,1,0:T(8,128)S(1)}, u32[]{:S(2)}, u32[]{:S(2)}) collective-permute-start(f32[2,48,256]{2,1,0:T(8,128)} %shard_map.118), channel_id=1, source_target_pairs={{0,1},{1,0},{2,3},{3,2},{4,5},{5,4},{6,7},{7,6},{8,9},{9,8},{10,11... | collective-permute-start | bytes 294920 | tf_op jit(solution)/shard_map/ppermute | solution.py:287
  16.2 0.0 copy-done
  16.2 0.1 copy.24
  16.3 0.1 copy.32
  16.4 0.8 convert_bitcast_fusion.w1f_ref
  17.3 0.1 stack.37
  17.4 0.1 stack.39
  17.5 0.1 stack.38
  17.7 0.1 copy.29
  17.9 0.7 pad.17.clone.w1t_ref
  18.6 0.7 pad.18.w2t_ref
  19.3 0.0 copy-done.3
  19.3 0.9 fusion.6.w1_ref
  20.3 0.6 fusion.17.vec_ref
  20.9 0.0 collective-permute-done
  20.9 0.9 fusion.10
  21.7 0.6 pad_maximum_fusion.stat_ref
  22.4 82.9 %shard_map.119 = (bf16[196,48,512]{2,1,0:T(8,128)(2,1)}, f32[2,48,256]{2,1,0:T(8,128)}, f32[512,208]{1,0:T(8,128)}, f32[512,208]{1,0:T(8,128)}) custom-call(bf16[196,48,512]{2,1,0:T(8,128)(2,1)} %bitcast.21, bf16[196,48,512]{2,1,0:T(8,128)(2,1)} %bitcast.23, f32[2,48,256]{2,1,0:T(8,128)} %pad_maximum_fusion.stat_ref, f32[1,512]{1,0:T(1,128)} %bitcast.29, ...), custom_call_target="tpu_custom_call" | custom-call | tf_op jit(solution)/shard_map/pallas_call | solution.py:340
  105.2 0.2 collective-permute-start.1
  105.4 4.7 %collective-permute-done.1 = f32[2,48,256]{2,1,0:T(8,128)S(1)} collective-permute-done((f32[2,48,256]{2,1,0:T(8,128)}, f32[2,48,256]{2,1,0:T(8,128)S(1)}, u32[]{:S(2)}, u32[]{:S(2)}) %collective-permute-start.1) | collective-permute-done | bytes 98336 | tf_op jit(solution)/shard_map/ppermute | solution.py:287
  110.1 1.5 add_multiply_fusion.sums_ref
  111.7 20.9 %shard_map.120 = (bf16[196,48,512]{2,1,0:T(8,128)(2,1)}, f32[2,512]{1,0:T(2,128)}) custom-call(bf16[196,48,512]{2,1,0:T(8,128)(2,1)} %bitcast.22, bf16[196,48,512]{2,1,0:T(8,128)(2,1)} %bitcast.24, bf16[196,48,512]{2,1,0:T(8,128)(2,1)} %get-tuple-element.14.gm_ref, f32[2,48,256]{2,1,0:T(8,128)} %pad_maximum_fusion.stat_ref, ...), custom_call_target="tpu_custom_call" | custom-call | flops 57802752 | bytes 38535168 | tf_op jit(solution)/shard_map/pallas_call | solution.py:373
  132.5 20.9 %shard_map.121 = (f32[2,32,208]{2,1,0:T(8,128)}, f32[2,512]{1,0:T(2,128)}) custom-call(f32[8,2,32,208]{3,2,1,0:T(8,128)} %bitcast.27, f32[8,2,32,208]{3,2,1,0:T(8,128)} %bitcast.28, f32[2,512]{1,0:T(2,128)} %get-tuple-element.19.chan_ref), custom_call_target="tpu_custom_call" | custom-call | tf_op jit(solution)/shard_map/pallas_call | solution.py:262
  153.5 1.4 slice_reduce_fusion
  154.9 1.4 multiply_bitcast_fusion.1
  156.3 1.3 fusion.20
  (7 shorter events, 0.1 us)
Async XLA Ops:
  0.6 15.5 %copy-start = (bf16[512,196]{0,1:T(8,128)(2,1)S(1)}, bf16[512,196]{0,1:T(8,128)(2,1)}, u32[]{:S(2)}) copy-start(bf16[512,196]{0,1:T(8,128)(2,1)} %param.10) | copy-start | bytes 602116
  0.6 16.6 %copy-start.4 = (f32[512]{0:T(512)S(1)}, f32[512]{0:T(512)}, u32[]{:S(2)}) copy-start(f32[512]{0:T(512)} %param.11) | copy-start | bytes 6148
  0.7 17.0 %copy-start.1 = (bf16[196,512]{1,0:T(8,128)(2,1)S(1)}, bf16[196,512]{1,0:T(8,128)(2,1)}, u32[]{:S(2)}) copy-start(bf16[196,512]{1,0:T(8,128)(2,1)} %param.12) | copy-start | bytes 602116
  0.7 18.6 %copy-start.3 = (f32[512]{0:T(512)S(1)}, f32[512]{0:T(512)}, u32[]{:S(2)}) copy-start(f32[512]{0:T(512)} %param.9) | copy-start | bytes 6148
  0.7 18.6 %copy-start.2 = (f32[512]{0:T(512)S(1)}, f32[512]{0:T(512)}, u32[]{:S(2)}) copy-start(f32[512]{0:T(512)} %param.8) | copy-start | bytes 6148
  13.2 7.7 %collective-permute-start = (f32[2,48,256]{2,1,0:T(8,128)}, f32[2,48,256]{2,1,0:T(8,128)S(1)}, u32[]{:S(2)}, u32[]{:S(2)}) collective-permute-start(f32[2,48,256]{2,1,0:T(8,128)} %shard_map.118), channel_id=1, source_target_pairs={{0,1},{1,0},{2,3},{3,2},{4,5},{5,4},{6,7},{7,6},{8,9},{9,8},{10,11... | collective-permute-start | bytes 294920 | tf_op jit(solution)/shard_map/ppermute | solution.py:287
  105.2 4.9 %collective-permute-start.1 = (f32[2,48,256]{2,1,0:T(8,128)}, f32[2,48,256]{2,1,0:T(8,128)S(1)}, u32[]{:S(2)}, u32[]{:S(2)}) collective-permute-start(f32[2,48,256]{2,1,0:T(8,128)} %get-tuple-element.15), channel_id=1, source_target_pairs={{0,1},{1,0},{2,3},{3,2},{4,5},{5,4},{6,7},{7,6},{8,9},{9,8},{10,11... | collective-permute-start | bytes 294920 | tf_op jit(solution)/shard_map/ppermute | solution.py:287

commit v2 on v1

--- a/solution.py
+++ b/solution.py
@@ -10,6 +10,7 @@
 epsilon = 1e-06
 T = 16
 LANES = 256
+SIDE = 128
 MIB = 2**20
 
 
@@ -27,17 +28,50 @@
     def _():
         out_ref[...] = jnp.zeros_like(out_ref)
 
+    f32 = jnp.float32
+    rows = x_ref.shape[0]
+    x = x_ref[...].reshape(rows * images, chans)
+    mean = jnp.dot(x, jnp.ones((chans, SIDE), jnp.bfloat16), preferred_element_type=f32)
+    mean = mean * (1.0 / chans)
+    square = jnp.zeros_like(mean)
+    for k in range(0, chans, SIDE):
+        d = x[:, k : k + SIDE].astype(f32) - mean
+        square = square + d * d
+    high = square.astype(jnp.bfloat16)
+    low = (square - high.astype(f32)).astype(jnp.bfloat16)
+    ones = jnp.ones((SIDE, SIDE), jnp.bfloat16)
+    square = jnp.dot(high, ones, preferred_element_type=f32) + jnp.dot(
+        low, ones, preferred_element_type=f32
+    )
     means, squares = out_ref[0], out_ref[1]
-    rows = x_ref.shape[0]
     for j in range(rows):
-        x = x_ref[j].astype(jnp.float32)
-        mean = jnp.sum(x, axis=-1, keepdims=True) * (1.0 / chans)
-        d = x - mean
-        square = jnp.sum(d * d, axis=-1, keepdims=True)
-        means = column(lane, i * rows + j, mean, means)
-        squares = column(lane, i * rows + j, square, squares)
+        part = slice(j * images, (j + 1) * images)
+        m = jnp.concatenate([mean[part]] * (LANES // SIDE), axis=1)
+        q = jnp.concatenate([square[part]] * (LANES // SIDE), axis=1)
+        means = column(lane, i * rows + j, m, means)
+        squares = column(lane, i * rows + j, q, squares)
     out_ref[0] = means
     out_ref[1] = squares
+
+
+def spread(value, count, chans):
+    f32 = jnp.float32
+    n = value.shape[0]
+    v = value[:, :SIDE]
+    lane = lax.broadcasted_iota(jnp.int32, v.shape, 1)
+    high = v.astype(jnp.bfloat16).astype(f32)
+    middle = (v - high).astype(jnp.bfloat16).astype(f32)
+    low = v - high - middle
+    placed = jnp.where(lane < 64, pltpu.roll(middle, 32, 1), pltpu.roll(low, 64, 1))
+    placed = jnp.where(lane < 32, high, placed)
+    lane = jnp.where(lane < 96, lax.rem(lane, 32), 32)
+    picks = [jnp.where(lane == j, placed, 0.0).astype(jnp.bfloat16) for j in range(count)]
+    ones = jnp.ones((SIDE, SIDE), jnp.bfloat16)
+    out = jnp.dot(jnp.concatenate(picks, axis=0), ones, preferred_element_type=f32)
+    return [
+        jnp.concatenate([out[j * n : (j + 1) * n]] * (chans // SIDE), axis=1)
+        for j in range(count)
+    ]
 
 
 def main_kernel(
@@ -78,9 +112,10 @@
 
     def prepare(first, count, mean, inv):
         rows = []
+        mean, inv = spread(mean, count, chans), spread(inv, count, chans)
         for j in range(count):
             x = x_ref[first + j].astype(f32)
-            normed = (x - mean[:, j : j + 1]) * inv[:, j : j + 1]
+            normed = (x - mean[j]) * inv[j]
             rows.append((normed * gain + bias).astype(jnp.bfloat16))
         return rows
 
@@ -98,7 +133,8 @@
     start = full * T
     one = jnp.ones((images, chans), jnp.bfloat16)
     zero = jnp.zeros((images, chans), jnp.bfloat16)
-    rows = prepare(start, tail, stat_ref[0, :, start:], stat_ref[1, :, start:]) + [one] * 3
+    rows = prepare(start, tail, rolled(full, 0), rolled(full, 1)) if tail else []
+    rows = rows + [one] * 3
     rows = rows + [zero] * (padded - start - len(rows))
     mixed[:, start:padded, :] = jnp.swapaxes(jnp.stack(rows), 0, 1)
     ups = [up_ref[start + j] for j in range(tail)]
@@ -160,19 +196,22 @@
         chan_ref[...] = jnp.zeros_like(chan_ref)
 
     shift = lax.rem(width - i * rows, width)
-    mean, inv = pltpu.roll(stat_ref[0], shift, 1), pltpu.roll(stat_ref[1], shift, 1)
-    s1, s2 = pltpu.roll(sums_ref[0], shift, 1), pltpu.roll(sums_ref[1], shift, 1)
+    chans = x_ref.shape[2]
+    raw = pltpu.roll(stat_ref[1], shift, 1)
+    mean = spread(pltpu.roll(stat_ref[0], shift, 1), rows, chans)
+    inv = spread(raw, rows, chans)
+    s1 = spread(raw * pltpu.roll(sums_ref[0], shift, 1), rows, chans)
+    s2 = spread(raw * pltpu.roll(sums_ref[1], shift, 1), rows, chans)
     products = jnp.zeros(x_ref.shape[1:], jnp.float32)
     plain = jnp.zeros(x_ref.shape[1:], jnp.float32)
     for j in range(rows):
-        c = slice(j, j + 1)
         x = x_ref[j].astype(jnp.float32)
-        normed = (x - mean[:, c]) * inv[:, c]
+        normed = (x - mean[j]) * inv[j]
         t = gm_ref[j].astype(jnp.float32)
         products = products + t * normed
         plain = plain + t
-        inner = t * gain - s1[:, c] - normed * s2[:, c]
-        out_ref[j] = (up_ref[j].astype(jnp.float32) + inv[:, c] * inner).astype(jnp.bfloat16)
+        inner = t * gain * inv[j] - s1[j] - normed * s2[j]
+        out_ref[j] = (up_ref[j].astype(jnp.float32) + inner).astype(jnp.bfloat16)
     chan_ref[0:1, :] += jnp.sum(products, axis=0, keepdims=True)
     chan_ref[1:2, :] += jnp.sum(plain, axis=0, keepdims=True)
 

time: 160 us -> 169 us (1.056)
  Pallas kernels: 137 us -> 146 us
    pallas_call x1, Pallas kernels: 82.9 us -> 88.1 us  [per_device(): pl.pallas_call(functools.partial(main_kernel, patches), grid=(batch // gr...]
    pallas_call x1, Pallas kernels: 12.5 us -> 14.6 us  [per_device(): pl.pallas_call(stats_kernel, grid=(steps,), in_specs=[pl.BlockSpec((rows,...]
where the time goes in v2:
time: 169 us; the launch traced here: 167 us
  Pallas kernels  146 us (86%)
  other arithmetic  6.87 us (4%)
  local copies, waits for them, and re-layouts  5 us (3%)
  waiting for transfers between devices  4.73 us (3%)
  starting transfers between devices  3.14 us (2%)
    pallas_call x1, Pallas kernels, per_device(): pl.pallas_call(functools.partial(main_kernel, patches), grid=(batch // gr...  88.1 us
    pallas_call x1, Pallas kernels, per_device(): pl.pallas_call(final_kernel, grid=(steps,), in_specs=[pblock, pblock, pbl...  22.4 us
    pallas_call x1, Pallas kernels, reduce_all(): pl.pallas_call(functools.partial(reduce_kernel, scale), in_specs=[vmem] *...  20.9 us
    pallas_call x1, Pallas kernels, per_device(): pl.pallas_call(stats_kernel, grid=(steps,), in_specs=[pl.BlockSpec((rows,...  14.6 us
    ppermute x2, waiting for transfers between devices, others(): lax.ppermute(x, axis, [(i, (i + s) % n) for i in range(n)])  4.73 us
  transfers between devices with their start and end apart: 2, of which 1 were waited for; matrix products, arithmetic and copies ran while one was open for 3% of the time, Pallas kernels for 0%

profile of v2, /device:TPU:0, one launch (start us, length us, event | category | flops | bytes accessed | tf_op | source)
XLA Modules:
  0.0 166.5 jit_solution(12440174295298452017)
XLA Ops:
  0.6 0.0 copy-start
  0.6 0.0 copy-start.4
  0.7 0.0 copy-start.1
  0.7 0.0 copy-start.3
  0.7 0.0 copy-start.2
  0.7 14.6 %shard_map.118 = f32[2,48,256]{2,1,0:T(8,128)} custom-call(bf16[196,48,512]{2,1,0:T(8,128)(2,1)} %bitcast.20), custom_call_target="tpu_custom_call" | custom-call | tf_op jit(solution)/shard_map/pallas_call | solution.py:345
  15.3 3.0 %collective-permute-start = (f32[2,48,256]{2,1,0:T(8,128)}, f32[2,48,256]{2,1,0:T(8,128)S(1)}, u32[]{:S(2)}, u32[]{:S(2)}) collective-permute-start(f32[2,48,256]{2,1,0:T(8,128)} %shard_map.118), channel_id=1, source_target_pairs={{0,1},{1,0},{2,3},{3,2},{4,5},{5,4},{6,7},{7,6},{8,9},{9,8},{10,11... | collective-permute-start | bytes 294920 | tf_op jit(solution)/shard_map/ppermute | solution.py:326
  18.3 0.1 copy.24
  18.4 0.1 copy.32
  18.6 0.8 convert_bitcast_fusion.w1f_ref
  19.4 0.0 copy-done.4
  19.4 0.1 stack.37
  19.5 0.1 stack.39
  19.7 0.1 stack.38
  19.8 0.1 copy.29
  20.0 0.7 pad.17.clone.w1t_ref
  20.7 0.7 pad.18.w2t_ref
  21.4 0.0 copy-done.2
  21.5 0.9 fusion.6.w1_ref
  22.4 0.6 fusion.17.vec_ref
  23.0 0.0 collective-permute-done
  23.0 0.9 fusion.10
  23.9 0.6 pad_maximum_fusion.stat_ref
  24.5 88.1 %shard_map.119 = (bf16[196,48,512]{2,1,0:T(8,128)(2,1)}, f32[2,48,256]{2,1,0:T(8,128)}, f32[512,208]{1,0:T(8,128)}, f32[512,208]{1,0:T(8,128)}) custom-call(bf16[196,48,512]{2,1,0:T(8,128)(2,1)} %bitcast.21, bf16[196,48,512]{2,1,0:T(8,128)(2,1)} %bitcast.23, f32[2,48,256]{2,1,0:T(8,128)} %pad_maximum_fusion.stat_ref, f32[1,512]{1,0:T(1,128)} %bitcast.29, ...), custom_call_target="tpu_custom_call" | custom-call | tf_op jit(solution)/shard_map/pallas_call | solution.py:379
  112.6 0.2 collective-permute-start.1
  112.8 4.7 %collective-permute-done.1 = f32[2,48,256]{2,1,0:T(8,128)S(1)} collective-permute-done((f32[2,48,256]{2,1,0:T(8,128)}, f32[2,48,256]{2,1,0:T(8,128)S(1)}, u32[]{:S(2)}, u32[]{:S(2)}) %collective-permute-start.1) | collective-permute-done | bytes 98336 | tf_op jit(solution)/shard_map/ppermute | solution.py:326
  117.5 1.5 add_multiply_fusion.sums_ref
  119.0 22.4 %shard_map.120 = (bf16[196,48,512]{2,1,0:T(8,128)(2,1)}, f32[2,512]{1,0:T(2,128)}) custom-call(bf16[196,48,512]{2,1,0:T(8,128)(2,1)} %bitcast.22, bf16[196,48,512]{2,1,0:T(8,128)(2,1)} %bitcast.24, bf16[196,48,512]{2,1,0:T(8,128)(2,1)} %get-tuple-element.14.gm_ref, f32[2,48,256]{2,1,0:T(8,128)} %pad_maximum_fusion.stat_ref, ...), custom_call_target="tpu_custom_call" | custom-call | flops 57802752 | bytes 38535168 | tf_op jit(solution)/shard_map/pallas_call | solution.py:412
  141.4 20.9 %shard_map.121 = (f32[2,32,208]{2,1,0:T(8,128)}, f32[2,512]{1,0:T(2,128)}) custom-call(f32[8,2,32,208]{3,2,1,0:T(8,128)} %bitcast.27, f32[8,2,32,208]{3,2,1,0:T(8,128)} %bitcast.28, f32[2,512]{1,0:T(2,128)} %get-tuple-element.19.chan_ref), custom_call_target="tpu_custom_call" | custom-call | tf_op jit(solution)/shard_map/pallas_call | solution.py:301
  162.4 1.4 slice_reduce_fusion
  163.8 1.4 multiply_bitcast_fusion.1
  165.2 1.3 fusion.20
  (7 shorter events, 0.1 us)
Async XLA Ops:
  0.6 17.7 %copy-start = (bf16[512,196]{0,1:T(8,128)(2,1)S(1)}, bf16[512,196]{0,1:T(8,128)(2,1)}, u32[]{:S(2)}) copy-start(bf16[512,196]{0,1:T(8,128)(2,1)} %param.10) | copy-start | bytes 602116
  0.6 18.8 %copy-start.4 = (f32[512]{0:T(512)S(1)}, f32[512]{0:T(512)}, u32[]{:S(2)}) copy-start(f32[512]{0:T(512)} %param.11) | copy-start | bytes 6148
  0.7 19.2 %copy-start.1 = (bf16[196,512]{1,0:T(8,128)(2,1)S(1)}, bf16[196,512]{1,0:T(8,128)(2,1)}, u32[]{:S(2)}) copy-start(bf16[196,512]{1,0:T(8,128)(2,1)} %param.12) | copy-start | bytes 602116
  0.7 20.8 %copy-start.3 = (f32[512]{0:T(512)S(1)}, f32[512]{0:T(512)}, u32[]{:S(2)}) copy-start(f32[512]{0:T(512)} %param.9) | copy-start | bytes 6148
  0.7 20.8 %copy-start.2 = (f32[512]{0:T(512)S(1)}, f32[512]{0:T(512)}, u32[]{:S(2)}) copy-start(f32[512]{0:T(512)} %param.8) | copy-start | bytes 6148
  15.3 7.7 %collective-permute-start = (f32[2,48,256]{2,1,0:T(8,128)}, f32[2,48,256]{2,1,0:T(8,128)S(1)}, u32[]{:S(2)}, u32[]{:S(2)}) collective-permute-start(f32[2,48,256]{2,1,0:T(8,128)} %shard_map.118), channel_id=1, source_target_pairs={{0,1},{1,0},{2,3},{3,2},{4,5},{5,4},{6,7},{7,6},{8,9},{9,8},{10,11... | collective-permute-start | bytes 294920 | tf_op jit(solution)/shard_map/ppermute | solution.py:326
  112.6 4.9 %collective-permute-start.1 = (f32[2,48,256]{2,1,0:T(8,128)}, f32[2,48,256]{2,1,0:T(8,128)S(1)}, u32[]{:S(2)}, u32[]{:S(2)}) collective-permute-start(f32[2,48,256]{2,1,0:T(8,128)} %get-tuple-element.15), channel_id=1, source_target_pairs={{0,1},{1,0},{2,3},{3,2},{4,5},{5,4},{6,7},{7,6},{8,9},{9,8},{10,11... | collective-permute-start | bytes 294920 | tf_op jit(solution)/shard_map/ppermute | solution.py:326

commit v3 on v1

--- a/solution.py
+++ b/solution.py
@@ -105,7 +105,7 @@
     ups = ups + [zero] * (padded - start - tail)
     upper[:, start:padded, :] = jnp.swapaxes(jnp.stack(ups), 0, 1)
 
-    block = 256
+    block = hidden
     across = (((1,), (1,)), ((), ()))
 
     def image(b, _):
@@ -136,7 +136,7 @@
         sums_ref[1, pl.ds(b, 1), :padded] = second - (dots[2:3] + dots[3:4])
         return 0
 
-    lax.fori_loop(0, images, image, 0)
+    lax.fori_loop(0, images, image, 0, unroll=2)
 
     def post(i, _):
         first = pl.multiple_of(i * T, T)
@@ -177,7 +177,9 @@
     chan_ref[1:2, :] += jnp.sum(plain, axis=0, keepdims=True)
 
 
-def reduce_kernel(scale, first_ref, second_ref, chan_ref, out_ref, chan_out_ref, *scratch):
+def reduce_kernel(scale, first_ref, second_ref, chan_ref, *rest):
+    first_out, second_out, bias_out, chan_out_ref, *scratch = rest
+    patches = first_out.shape[1]
     one, one_c, held, held_c, two, two_c, own, three, sems, sems2, sems3 = scratch
     me, col = lax.axis_index("dp"), lax.axis_index("chan")
     n_dp, n_chan = lax.axis_size("dp"), lax.axis_size("chan")
@@ -247,10 +249,12 @@
     total = three[0]
     for j in range(1, n_chan):
         total = total + three[j]
-    out_ref[...] = total * scale
-
-
-def reduce_all(first, second, chan, scale):
+    first_out[...] = total[0, :, :patches] * scale
+    second_out[...] = total[1, :, :patches] * (0.5 * scale)
+    bias_out[...] = total[0, :, patches : patches + 1] * scale
+
+
+def reduce_all(first, second, chan, patches, scale):
     n_dp, n_chan = lax.axis_size("dp"), lax.axis_size("chan")
     halves = n_dp // 2
     rows, lanes = first.shape[0] // n_dp, first.shape[1]
@@ -262,8 +266,13 @@
     return pl.pallas_call(
         functools.partial(reduce_kernel, scale),
         in_specs=[vmem] * 3,
-        out_specs=[vmem] * 2,
-        out_shape=[S((2, rows, lanes), f32), S(chan.shape, f32)],
+        out_specs=[vmem] * 4,
+        out_shape=[
+            S((rows, patches), f32),
+            S((rows, patches), f32),
+            S((rows, 1), f32),
+            S(chan.shape, f32),
+        ],
         scratch_shapes=[
             pltpu.VMEM((2, halves, rows, lanes), f32),
             pltpu.VMEM(chan.shape, f32),
@@ -389,15 +398,8 @@
         ),
     )(x, up, gm, stat, sums, gain2)
 
-    mine, chan = reduce_all(gf, gs, chan, scale)
-    return (
-        jnp.transpose(out, (1, 0, 2)),
-        mine[0, :, :patches],
-        (0.5 * mine[1, :, :patches]).T,
-        mine[0, :, patches],
-        chan[0],
-        chan[1],
-    )
+    first, second, bias, chan = reduce_all(gf, gs, chan, patches, scale)
+    return (jnp.transpose(out, (1, 0, 2)), first, second.T, bias[:, 0], chan[0], chan[1])
 
 
 def solution(mesh):

time: 160 us -> 154 us (0.963)
  Pallas kernels: 137 us -> 129 us
    pallas_call x1, Pallas kernels: 82.9 us -> 75 us  [per_device(): pl.pallas_call(functools.partial(main_kernel, patches), grid=(batch // gr...]
    unnamed x13 -> x15, local copies, waits for them, and re-layouts: 0.42 us -> 3.16 us
where the time goes in v3:
time: 154 us; the launch traced here: 151 us
  Pallas kernels  129 us (84%)
  other arithmetic  6.81 us (4%)
  local copies, waits for them, and re-layouts  6.36 us (4%)
  waiting for transfers between devices  4.74 us (3%)
  starting transfers between devices  3.12 us (2%)
    pallas_call x1, Pallas kernels, per_device(): pl.pallas_call(functools.partial(main_kernel, patches), grid=(batch // gr...  75 us
    pallas_call x1, Pallas kernels, reduce_all(): pl.pallas_call(functools.partial(reduce_kernel, scale), in_specs=[vmem] *...  21 us
    pallas_call x1, Pallas kernels, per_device(): pl.pallas_call(final_kernel, grid=(steps,), in_specs=[pblock, pblock, pbl...  20.9 us
    pallas_call x1, Pallas kernels, per_device(): pl.pallas_call(stats_kernel, grid=(steps,), in_specs=[pl.BlockSpec((rows,...  12.5 us
    ppermute x2, waiting for transfers between devices, others(): lax.ppermute(x, axis, [(i, (i + s) % n) for i in range(n)])  4.74 us
    unnamed x15, local copies, waits for them, and re-layouts  3.16 us
    ppermute x2, starting transfers between devices, others(): lax.ppermute(x, axis, [(i, (i + s) % n) for i in range(n)])  3.12 us
  transfers between devices with their start and end apart: 2, of which 1 were waited for; matrix products, arithmetic and copies ran while one was open for 3% of the time, Pallas kernels for 0%

profile of v3, /device:TPU:0, one launch (start us, length us, event | category | flops | bytes accessed | tf_op | source)
XLA Modules:
  0.0 151.1 jit_solution(10414096335294702554)
XLA Ops:
  0.6 0.0 copy-start
  0.6 0.0 copy-start.4
  0.7 0.0 copy-start.1
  0.7 0.0 copy-start.3
  0.7 0.0 copy-start.2
  0.7 12.5 %shard_map.118 = f32[2,48,256]{2,1,0:T(8,128)} custom-call(bf16[196,48,512]{2,1,0:T(8,128)(2,1)} %bitcast.15), custom_call_target="tpu_custom_call" | custom-call | tf_op jit(solution)/shard_map/pallas_call | solution.py:315
  13.2 3.0 %collective-permute-start = (f32[2,48,256]{2,1,0:T(8,128)}, f32[2,48,256]{2,1,0:T(8,128)S(1)}, u32[]{:S(2)}, u32[]{:S(2)}) collective-permute-start(f32[2,48,256]{2,1,0:T(8,128)} %shard_map.118), channel_id=1, source_target_pairs={{0,1},{1,0},{2,3},{3,2},{4,5},{5,4},{6,7},{7,6},{8,9},{9,8},{10,11... | collective-permute-start | bytes 294920 | tf_op jit(solution)/shard_map/ppermute | solution.py:296
  16.2 0.1 copy.24
  16.3 0.1 copy.32
  16.4 0.8 convert_bitcast_fusion.w1f_ref
  17.3 0.1 stack.37
  17.4 0.1 stack.39
  17.6 0.1 stack.38
  17.7 0.1 copy.29
  17.9 0.7 pad.17.clone.w1t_ref
  18.6 0.7 pad.18.w2t_ref
  19.3 0.0 copy-done.3
  19.4 0.9 fusion.6.w1_ref
  20.3 0.6 fusion.17.vec_ref
  20.9 0.0 collective-permute-done
  20.9 0.9 fusion.10
  21.8 0.6 pad_maximum_fusion.stat_ref
  22.4 75.0 %shard_map.119 = (bf16[196,48,512]{2,1,0:T(8,128)(2,1)}, f32[2,48,256]{2,1,0:T(8,128)}, f32[512,208]{1,0:T(8,128)}, f32[512,208]{1,0:T(8,128)}) custom-call(bf16[196,48,512]{2,1,0:T(8,128)(2,1)} %bitcast.16, bf16[196,48,512]{2,1,0:T(8,128)(2,1)} %bitcast.18, f32[2,48,256]{2,1,0:T(8,128)} %pad_maximum_fusion.stat_ref, f32[1,512]{1,0:T(1,128)} %bitcast.25, ...), custom_call_target="tpu_custom_call" | custom-call | tf_op jit(solution)/shard_map/pallas_call | solution.py:349
  97.4 0.2 collective-permute-start.1
  97.6 4.7 %collective-permute-done.1 = f32[2,48,256]{2,1,0:T(8,128)S(1)} collective-permute-done((f32[2,48,256]{2,1,0:T(8,128)}, f32[2,48,256]{2,1,0:T(8,128)S(1)}, u32[]{:S(2)}, u32[]{:S(2)}) %collective-permute-start.1) | collective-permute-done | bytes 98336 | tf_op jit(solution)/shard_map/ppermute | solution.py:296
  102.3 1.6 %add_multiply_fusion.sums_ref = f32[2,48,256]{2,1,0:T(8,128)} fusion(f32[2,48,256]{2,1,0:T(8,128)} %get-tuple-element.17, f32[2,48,256]{2,1,0:T(8,128)S(1)} %collective-permute-done.1), kind=kLoop, calls=%fused_computation.11 | loop fusion | flops 49152 | bytes 294912 | tf_op jit(solution)/shard_map/div | solution.py:379
  103.9 20.9 %shard_map.120 = (bf16[196,48,512]{2,1,0:T(8,128)(2,1)}, f32[2,512]{1,0:T(2,128)}) custom-call(bf16[196,48,512]{2,1,0:T(8,128)(2,1)} %bitcast.17, bf16[196,48,512]{2,1,0:T(8,128)(2,1)} %bitcast.19, bf16[196,48,512]{2,1,0:T(8,128)(2,1)} %get-tuple-element.16.gm_ref, f32[2,48,256]{2,1,0:T(8,128)} %pad_maximum_fusion.stat_ref, ...), custom_call_target="tpu_custom_call" | custom-call | flops 57802752 | bytes 38535168 | tf_op jit(solution)/shard_map/pallas_call | solution.py:382
  124.7 21.0 %shard_map.121 = (f32[32,196]{1,0:T(8,128)}, f32[32,196]{1,0:T(8,128)}, f32[32,1]{1,0:T(8,128)}, f32[2,512]{1,0:T(2,128)}) custom-call(f32[8,2,32,208]{3,2,1,0:T(8,128)} %bitcast.22, f32[8,2,32,208]{3,2,1,0:T(8,128)} %bitcast.23, f32[2,512]{1,0:T(2,128)} %get-tuple-element.21.chan_ref), custom_call_target="tpu_custom_call" | custom-call | tf_op jit(solution)/shard_map/pallas_call | solution.py:266
  145.7 1.3 fusion.20
  147.0 1.3 reduce
  148.4 1.4 copy.35
  149.7 1.4 copy.36
  (8 shorter events, 0.1 us)
Async XLA Ops:
  0.6 15.5 %copy-start = (bf16[512,196]{0,1:T(8,128)(2,1)S(1)}, bf16[512,196]{0,1:T(8,128)(2,1)}, u32[]{:S(2)}) copy-start(bf16[512,196]{0,1:T(8,128)(2,1)} %param.10) | copy-start | bytes 602116
  0.6 16.6 %copy-start.4 = (f32[512]{0:T(512)S(1)}, f32[512]{0:T(512)}, u32[]{:S(2)}) copy-start(f32[512]{0:T(512)} %param.11) | copy-start | bytes 6148
  0.7 17.0 %copy-start.1 = (bf16[196,512]{1,0:T(8,128)(2,1)S(1)}, bf16[196,512]{1,0:T(8,128)(2,1)}, u32[]{:S(2)}) copy-start(bf16[196,512]{1,0:T(8,128)(2,1)} %param.12) | copy-start | bytes 602116
  0.7 18.7 %copy-start.3 = (f32[512]{0:T(512)S(1)}, f32[512]{0:T(512)}, u32[]{:S(2)}) copy-start(f32[512]{0:T(512)} %param.9) | copy-start | bytes 6148
  0.7 18.7 %copy-start.2 = (f32[512]{0:T(512)S(1)}, f32[512]{0:T(512)}, u32[]{:S(2)}) copy-start(f32[512]{0:T(512)} %param.8) | copy-start | bytes 6148
  13.2 7.7 %collective-permute-start = (f32[2,48,256]{2,1,0:T(8,128)}, f32[2,48,256]{2,1,0:T(8,128)S(1)}, u32[]{:S(2)}, u32[]{:S(2)}) collective-permute-start(f32[2,48,256]{2,1,0:T(8,128)} %shard_map.118), channel_id=1, source_target_pairs={{0,1},{1,0},{2,3},{3,2},{4,5},{5,4},{6,7},{7,6},{8,9},{9,8},{10,11... | collective-permute-start | bytes 294920 | tf_op jit(solution)/shard_map/ppermute | solution.py:296
  97.4 4.9 %collective-permute-start.1 = (f32[2,48,256]{2,1,0:T(8,128)}, f32[2,48,256]{2,1,0:T(8,128)S(1)}, u32[]{:S(2)}, u32[]{:S(2)}) collective-permute-start(f32[2,48,256]{2,1,0:T(8,128)} %get-tuple-element.17), channel_id=1, source_target_pairs={{0,1},{1,0},{2,3},{3,2},{4,5},{5,4},{6,7},{7,6},{8,9},{9,8},{10,11... | collective-permute-start | bytes 294920 | tf_op jit(solution)/shard_map/ppermute | solution.py:296
